TPU v7x, 512 devices: a 8x2x16 block of a 8x8x16 slice. The times are simulated.
512 devices in a mesh: groups: 2 (over y), range: 128 (over z, x), sub: 2 (over core).
Axes of the slice: x: 8, y: 2, z: 16, core: 2. Of those that a mesh axis runs over, the one named last changes fastest.
The devices are a block of a 8x8x16 slice.
Arguments:
- samples: float32 [2, 1024, 512, 128], P(None, ('groups', 'range', 'sub')), parts along dimension 1, may hold values from -6 to 6
- beam_weights: float32 [512, 8, 2, 64, 128], P(('groups', 'range'), None, None, None, 'sub'), parts along dimension 0, may hold values from -0.25 to 0.25
- subarrays: int32 [512, 8, 64], P(('groups', 'range', 'sub')), parts along dimension 0, may hold values from 0 to 511, as said below
- training: int32 [1024], P(('groups', 'range', 'sub')), parts along dimension 0, may hold values 0 or 1
Outputs:
- covariance: float32 [512, 8, 64, 128], P(('groups', 'range', 'sub')), parts along dimension 0
- filtered: float32 [2, 128, 1024, 128], P(None, None, ('groups', 'range', 'sub')), parts along dimension 2
- energy: float32 [256], P('groups'), parts along dimension 0
There are 2 independent parts, one for each index of `groups`. A program takes and returns all parts, laid end to end along the dimension named above; each array names one. Nothing has to cross between parts.
Inputs may be any that keep to these rules, and one draw needn't show every extreme that they name: `subarrays`: in each gate block the 512 indices are all 512 channels, each once.
All inputs are finite; a program needn't handle non-finite values. No bound on the sum of `training` on one device may be relied on, other than what follows from the above.
Results may differ from a plain program's by a relative error of at most 0.0003.
Values sent between devices are 32-bit elements; how exact they have to be, the bound alone decides.
A program may use at most 64 MiB of HBM per device.

v0:
```python
import functools
import jax
import jax.numpy as jnp
from jax import lax
from jax.sharding import Mesh
from jax.sharding import PartitionSpec as P

GB = 2
RANGE = ("range_0", "range_1")
RANGE_SUB = ("range_0", "range_1", "sub")
GROUPS_RANGE_SUB = ("groups", "range_0", "range_1", "sub")
GROUPS_RANGE = ("groups", "range_0", "range_1")
loading = 0.05


def split_up(array, dim, peers):
    lengths = array.shape
    parts = array.reshape(*lengths[:dim], peers, lengths[dim] // peers, *lengths[dim + 1 :])
    return jnp.moveaxis(parts, dim, 0)


def joined_along(parts, dim):
    lengths = list(parts.shape[1:])
    lengths[dim] *= parts.shape[0]
    return jnp.moveaxis(parts, 0, dim).reshape(lengths)


def one_exchange(array, axis, axes, splits, concats):
    sizes = [lax.axis_size(a) for a in axes]
    parts = split_up(array, splits[0], sizes[0])
    parts = jnp.moveaxis(split_up(parts, splits[1] + 1, sizes[1]), 0, 1)
    inside = parts.shape[2:]
    parts = parts.reshape(-1, *inside)
    parts = lax.all_to_all(parts, axis, split_axis=0, concat_axis=0, tiled=True)
    parts = joined_along(parts.reshape(*sizes, *inside), concats[0] + 1)
    return joined_along(parts, concats[1])


def by_axis(array, axes):
    return functools.reduce(lax.psum, axes, array)


def block_terms(snaps, chosen, weights, masked, factor):
    highest = lax.Precision.HIGHEST
    picked = jnp.take(snaps, chosen, axis=1)
    real_part = picked[0]
    imag_part = picked[1]
    real_masked = real_part * masked
    imag_masked = imag_part * masked
    cov_real = (
        jnp.einsum("snx,smx->snm", real_masked, real_part, precision=highest)
        + jnp.einsum("snx,smx->snm", imag_masked, imag_part, precision=highest)
    ) * factor
    cov_imag = (
        jnp.einsum("snx,smx->snm", imag_masked, real_part, precision=highest)
        - jnp.einsum("snx,smx->snm", real_masked, imag_part, precision=highest)
    ) * factor
    w_real = weights[:, 0]
    w_imag = weights[:, 1]
    out_real = jnp.einsum("snk,snx->kx", w_real, real_part, precision=highest) + jnp.einsum(
        "snk,snx->kx", w_imag, imag_part, precision=highest
    )
    out_imag = jnp.einsum("snk,snx->kx", w_real, imag_part, precision=highest) - jnp.einsum(
        "snk,snx->kx", w_imag, real_part, precision=highest
    )
    prod_real = jnp.einsum("snm,smk->snk", cov_real, w_real, precision=highest) - jnp.einsum(
        "snm,smk->snk", cov_imag, w_imag, precision=highest
    )
    prod_imag = jnp.einsum("snm,smk->snk", cov_real, w_imag, precision=highest) + jnp.einsum(
        "snm,smk->snk", cov_imag, w_real, precision=highest
    )
    quadratic = jnp.sum(w_real * prod_real + w_imag * prod_imag, axis=(0, 1))
    inverse = 1.0 / jnp.sqrt(quadratic + loading)
    filtered = jnp.stack([out_real * inverse[:, None], out_imag * inverse[:, None]])
    energy = jnp.sum(out_real * out_real + out_imag * out_imag, axis=1)
    covariance = jnp.concatenate([cov_real, cov_imag], axis=-1)
    return (covariance, filtered, energy)


def body(samples, beam_weights, subarrays, training):
    range_count = lax.axis_size(RANGE)
    core_count = lax.axis_size("sub")
    parts_iq, chan_dev, all_gates, pulses = samples.shape
    gate_dev = all_gates // (range_count * core_count)
    channels = chan_dev * range_count * core_count
    blocks_dev = gate_dev // GB
    spread = samples.reshape(parts_iq, 1, 1, chan_dev, range_count, core_count, gate_dev, pulses)
    turned = one_exchange(spread, RANGE_SUB, (RANGE, "sub"), (4, 5), (1, 2))
    local_data = turned.reshape(parts_iq, channels, blocks_dev, GB * pulses).transpose(2, 0, 1, 3)
    mine = lax.all_to_all(beam_weights, "sub", split_axis=0, concat_axis=4, tiled=True)
    gates_on = training.astype(jnp.float32).reshape(blocks_dev, GB)
    masked = jnp.repeat(gates_on, pulses, axis=1)
    factor = 1.0 / (GB * pulses)
    covs, filts, energies = jax.vmap(block_terms, in_axes=(0, 0, 0, 0, None))(
        local_data, subarrays, mine, masked, factor
    )
    beams = filts.shape[2]
    filtered = filts.reshape(blocks_dev, parts_iq, beams, GB, pulses).transpose(1, 2, 0, 3, 4)
    filtered = filtered.reshape(parts_iq, beams, gate_dev, pulses)
    total = by_axis(jnp.sum(energies, axis=0), RANGE_SUB)
    energy = total / (all_gates * pulses)
    return (covs, filtered, energy)


def solution(mesh):
    torus = Mesh(
        mesh.devices.reshape(mesh.shape["groups"], 16, 8, mesh.shape["sub"]),
        ("groups", "range_0", "range_1", "sub"),
    )
    placed = (
        P(None, GROUPS_RANGE_SUB, None, None),
        P(GROUPS_RANGE, None, None, None, "sub"),
        P(GROUPS_RANGE_SUB, None, None),
        P(GROUPS_RANGE_SUB),
    )
    return jax.shard_map(
        body,
        mesh=torus,
        in_specs=placed,
        out_specs=(
            P(GROUPS_RANGE_SUB, None, None, None),
            P(None, None, GROUPS_RANGE_SUB, None),
            P("groups"),
        ),
        check_vma=False,
    )
```

profile of v0, /device:TPU:65, one launch (start us, length us, event | category | flops | bytes accessed | tf_op | source)
XLA Modules:
  0.0 181.8 jit_solution(4154683008116402408)
XLA Ops:
  0.6 0.0 copy-start
  0.6 2.5 %reshape.168 = f32[2,1,65536]{2,1,0:T(1,128)} reshape(f32[2,8,2,64,64]{4,3,2,1,0:T(8,128)} %param.5) | data formatting | bytes 1048576
  3.2 44.9 %all-to-all-start.1 = ((f32[2,1,65536]{2,1,0:T(1,128)}), f32[2,1,65536]{2,1,0:T(1,128)S(1)}, u32[]{:S(2)}, u32[]{:S(2)}) async-start(f32[2,1,65536]{2,1,0:T(1,128)} %reshape.168), calls=%async_computation.1 | async-start | bytes 1048576 | tf_op jit(solution)/shard_map/all_to_all | solution.py:90
  48.1 0.0 copy-done
  48.1 1.3 copy.16
  49.4 0.0 all-to-all-done.1
  49.4 0.0 copy-start.2
  49.5 0.0 copy-start.1
  49.5 16.2 %all-to-all-start = ((f32[256,2,1,1,2,1,1,2,128]{8,7,4,1,6,5,3,2,0:T(2,128)}), f32[256,2,1,1,2,1,1,2,128]{8,7,4,1,6,5,3,2,0:T(2,128)S(1)}, u32[]{:S(2)}, u32[]{:S(2)}) async-start(f32[256,2,1,1,2,1,1,2,128]{8,7,4,1,6,5,3,2,0:T(2,128)} %bitcast.5), calls=%async_computation | async-start | bytes 2097152 | tf_op jit(solution)/shard_map/all_to_all | solution.py:34
  65.7 0.0 copy-done.2
  65.7 0.0 copy-done.1
  65.7 0.1 reshape.158
  65.8 0.5 broadcast.75
  66.3 2.3 %reduce.5 = f32[2,65536]{1,0:T(2,128)S(1)} reduce(f32[2,1,65536]{2,1,0:T(1,128)S(1)} %all-to-all-done.1, f32[]{:T(128)} %broadcast.75), dimensions={1}, to_apply=%all_to_all.17.reduce_sub_computation | reduce | bytes 1048580 | tf_op jit(solution)/shard_map/all_to_all | solution.py:90
  68.6 0.6 reshape.169
  69.3 1.9 %copy.20 = f32[1,8,2,64,2,64]{5,4,3,1,2,0:T(2,128)} copy(f32[1,8,2,64,2,64]{5,3,2,1,4,0:T(8,128)S(1)} %bitcast.104) | data formatting | bytes 1048576 | tf_op jit(solution)/shard_map/all_to_all | solution.py:90
  71.1 1.8 all_to_all.20
  72.9 0.1 broadcast_bitcast_fusion
  73.0 48.2 %all-to-all-done = f32[256,2,1,1,2,1,1,2,128]{8,7,4,1,6,5,3,2,0:T(2,128)S(1)} async-done(((f32[256,2,1,1,2,1,1,2,128]{8,7,4,1,6,5,3,2,0:T(2,128)}), f32[256,2,1,1,2,1,1,2,128]{8,7,4,1,6,5,3,2,0:T(2,128)S(1)}, u32[]{:S(2)}, u32[]{:S(2)}) %all-to-all-start) | async-done | bytes 1048608 | tf_op jit(solution)/shard_map/all_to_all | solution.py:34
  121.3 0.4 copy.17
  121.6 0.8 copy.18
  122.4 2.6 %gather_fusion = f32[512,2,256]{2,1,0:T(2,128)S(1)} fusion(f32[1,2,512,256]{3,1,2,0:T(2,128)S(1)} %copy.18, s32[512]{0:T(512)S(1)} %reshape.158), kind=kCustom, calls=%fused_computation | custom fusion | bytes 2101248 | tf_op jit(solution)/shard_map/vmap(jit(_take))/gather | solution.py:45
  125.0 0.1 copy.19
  125.1 0.1 broadcast_select_fusion
  125.2 1.0 convolution_bitcast_fusion.2
  126.2 1.0 convolution_bitcast_fusion
  127.2 0.6 fusion.12
  127.9 0.6 fusion.2
  128.5 0.4 fusion.19
  128.9 0.4 fusion.18
  129.3 0.6 fusion.8
  129.9 1.0 fusion.6
  130.9 0.6 fusion.3
  131.6 0.4 fusion
  132.0 0.4 fusion.5
  132.4 1.0 add_reduce_fusion
  133.5 20.4 %psum.21 = f32[128]{0:T(128)S(1)} all-reduce(f32[128]{0:T(128)S(1)} %get-tuple-element.3), channel_id=1, replica_groups=mesh['groups'=2,'range_0'=16,'range_1'=8,'sub'=2] {'range_0'}, use_global_device_ids=true, to_apply=%region_2.3 | all-reduce | flops 128 | bytes 1024 | tf_op jit(solution)/shard_map/psum | solution.py:40
  153.8 11.9 %psum.22 = f32[128]{0:T(128)S(1)} all-reduce(f32[128]{0:T(128)S(1)} %psum.21), channel_id=1, replica_groups=mesh['groups'=2,'range_0'=16,'range_1'=8,'sub'=2] {'range_1'}, use_global_device_ids=true, to_apply=%region_3.4 | all-reduce | flops 128 | bytes 1024 | tf_op jit(solution)/shard_map/psum | solution.py:40
  165.7 13.7 %psum.23 = f32[128]{0:T(128)S(1)} all-reduce(f32[128]{0:T(128)S(1)} %psum.22), channel_id=1, replica_groups=mesh['groups'=2,'range_0'=16,'range_1'=8,'sub'=2] {'sub'}, use_global_device_ids=true, to_apply=%region_4.5 | all-reduce | flops 128 | bytes 1024 | tf_op jit(solution)/shard_map/psum | solution.py:40
  179.4 0.5 broadcast_multiply_fusion.2
  179.9 0.1 copy.21
  180.0 0.1 copy.22
  180.2 0.8 pad_maximum_fusion
  181.0 0.8 pad_maximum_fusion.1
  (6 shorter events, 0.0 us)
Async XLA Ops:
  0.6 47.4 %copy-start = (f32[2,2,512,128]{3,2,1,0:T(8,128)S(1)}, f32[2,2,512,128]{3,2,1,0:T(8,128)}, u32[]{:S(2)}) copy-start(f32[2,2,512,128]{3,2,1,0:T(8,128)} %param.4) | copy-start | bytes 3145732
  3.2 46.3 %all-to-all-start.1 = ((f32[2,1,65536]{2,1,0:T(1,128)}), f32[2,1,65536]{2,1,0:T(1,128)S(1)}, u32[]{:S(2)}, u32[]{:S(2)}) async-start(f32[2,1,65536]{2,1,0:T(1,128)} %reshape.168), calls=%async_computation.1 | async-start | bytes 1048576 | tf_op jit(solution)/shard_map/all_to_all | solution.py:90
  49.4 16.2 %copy-start.2 = (s32[2]{0:T(128)S(1)}, s32[2]{0:T(128)}, u32[]{:S(2)}) copy-start(s32[2]{0:T(128)} %param.7) | copy-start | bytes 28
  49.5 16.2 %copy-start.1 = (s32[1,8,64]{2,1,0:T(8,128)S(1)}, s32[1,8,64]{2,1,0:T(8,128)}, u32[]{:S(2)}) copy-start(s32[1,8,64]{2,1,0:T(8,128)} %param.6) | copy-start | bytes 6148
  49.5 71.8 %all-to-all-start = ((f32[256,2,1,1,2,1,1,2,128]{8,7,4,1,6,5,3,2,0:T(2,128)}), f32[256,2,1,1,2,1,1,2,128]{8,7,4,1,6,5,3,2,0:T(2,128)S(1)}, u32[]{:S(2)}, u32[]{:S(2)}) async-start(f32[256,2,1,1,2,1,1,2,128]{8,7,4,1,6,5,3,2,0:T(2,128)} %bitcast.5), calls=%async_computation | async-start | bytes 2097152 | tf_op jit(solution)/shard_map/all_to_all | solution.py:34
where the time goes:
time: 182 us
  starting transfers between devices  61.1 us (34%)
  waiting for transfers between devices  48.3 us (27%)
  blocking collectives  46 us (25%)
  local copies, waits for them, and re-layouts  12.9 us (7%)
  matrix products  8.12 us (4%)
  other arithmetic  4.67 us (3%)
    all_to_all x1, waiting for transfers between devices, one_exchange(): parts = lax.all_to_all(parts, axis, split_axis=0, concat_axis=0, tiled=True)  48.2 us
    psum x3, blocking collectives, by_axis(): return functools.reduce(lax.psum, axes, array)  46 us
    all_to_all x1, starting transfers between devices, body(): lax.all_to_all(beam_weights, 'sub', split_axis=0, concat_axis=4, tiled=True)  44.9 us
    all_to_all x1, starting transfers between devices, one_exchange(): parts = lax.all_to_all(parts, axis, split_axis=0, concat_axis=0, tiled=True)  16.2 us
    all_to_all x3, local copies, waits for them, and re-layouts, body(): lax.all_to_all(beam_weights, 'sub', split_axis=0, concat_axis=4, tiled=True)  4.18 us
  transfers between devices with their start and end apart: 2, of which 1 were waited for; matrix products, arithmetic and copies ran while one was open for 4% of the time, Pallas kernels for 0%

commit v1 on v0

--- a/solution.py
+++ b/solution.py
@@ -11,6 +11,12 @@
 GROUPS_RANGE_SUB = ("groups", "range_0", "range_1", "sub")
 GROUPS_RANGE = ("groups", "range_0", "range_1")
 loading = 0.05
+
+
+def exchange_blocks(x, axis, split, join):
+    pieces = jnp.split(x, lax.axis_size(axis), axis=split)
+    received = lax.all_to_all(jnp.stack(pieces), axis, 0, 0)
+    return jnp.concatenate(received, axis=join)
 
 
 def split_up(array, dim, peers):
@@ -87,7 +93,7 @@
     spread = samples.reshape(parts_iq, 1, 1, chan_dev, range_count, core_count, gate_dev, pulses)
     turned = one_exchange(spread, RANGE_SUB, (RANGE, "sub"), (4, 5), (1, 2))
     local_data = turned.reshape(parts_iq, channels, blocks_dev, GB * pulses).transpose(2, 0, 1, 3)
-    mine = lax.all_to_all(beam_weights, "sub", split_axis=0, concat_axis=4, tiled=True)
+    mine = exchange_blocks(beam_weights, "sub", 0, 4)
     gates_on = training.astype(jnp.float32).reshape(blocks_dev, GB)
     masked = jnp.repeat(gates_on, pulses, axis=1)
     factor = 1.0 / (GB * pulses)

time: 182 us -> 181 us (level)
    all_to_all x3 -> x1, local copies, waits for them, and re-layouts: 4.18 us -> 0.51 us  [exchange_blocks(): received = lax.all_to_all(jnp.stack(pieces), axis, 0, 0)]
    reshape x0 -> x2, local copies, waits for them, and re-layouts: none -> 3.67 us  [exchange_blocks(): return jnp.concatenate(received, axis=join)]
  transfers between devices with their start and end apart: 2 -> 2, of which waited for: 1 -> 1; matrix products, arithmetic and copies ran while one was open for 4% -> 5% of each run, Pallas kernels for 0% -> 0%
where the time goes in v1:
time: 181 us
  starting transfers between devices  61.1 us (34%)
  waiting for transfers between devices  47.7 us (26%)
  blocking collectives  46 us (25%)
  local copies, waits for them, and re-layouts  13.5 us (7%)
  matrix products  6.68 us (4%)
  other arithmetic  4.74 us (3%)
    all_to_all x1, waiting for transfers between devices, one_exchange(): parts = lax.all_to_all(parts, axis, split_axis=0, concat_axis=0, tiled=True)  47.7 us
    psum x3, blocking collectives, by_axis(): return functools.reduce(lax.psum, axes, array)  46 us
    all_to_all x1, starting transfers between devices, exchange_blocks(): received = lax.all_to_all(jnp.stack(pieces), axis, 0, 0)  44.9 us
    all_to_all x1, starting transfers between devices, one_exchange(): parts = lax.all_to_all(parts, axis, split_axis=0, concat_axis=0, tiled=True)  16.2 us
    reshape x2, local copies, waits for them, and re-layouts, exchange_blocks(): return jnp.concatenate(received, axis=join)  3.67 us
  transfers between devices with their start and end apart: 2, of which 1 were waited for; matrix products, arithmetic and copies ran while one was open for 5% of the time, Pallas kernels for 0%

profile of v1, /device:TPU:65, one launch (start us, length us, event | category | flops | bytes accessed | tf_op | source)
XLA Modules:
  0.0 180.6 jit_solution(14111805395530618673)
XLA Ops:
  0.6 1.3 slice_bitcast_fusion.3
  1.9 0.1 pad_maximum_fusion
  2.0 0.0 copy-start
  2.0 1.4 reshape.176
  3.4 44.9 %all-to-all-start.1 = ((f32[2,1,65536]{2,1,0:T(1,128)}), f32[2,1,65536]{2,1,0:T(1,128)S(1)}, u32[]{:S(2)}, u32[]{:S(2)}) async-start(f32[2,1,65536]{2,1,0:T(1,128)} %reshape.176), calls=%async_computation.1 | async-start | bytes 1048576 | tf_op jit(solution)/shard_map/all_to_all | solution.py:18
  48.4 0.0 copy-done
  48.4 1.3 copy.12
  49.7 0.0 all-to-all-done.1
  49.7 0.0 copy-start.1
  49.7 16.2 %all-to-all-start = ((f32[256,2,1,1,2,1,1,2,128]{8,7,4,1,6,5,3,2,0:T(2,128)}), f32[256,2,1,1,2,1,1,2,128]{8,7,4,1,6,5,3,2,0:T(2,128)S(1)}, u32[]{:S(2)}, u32[]{:S(2)}) async-start(f32[256,2,1,1,2,1,1,2,128]{8,7,4,1,6,5,3,2,0:T(2,128)} %bitcast.5), calls=%async_computation | async-start | bytes 2097152 | tf_op jit(solution)/shard_map/all_to_all | solution.py:40
  65.9 0.0 copy-done.1
  66.0 0.0 copy-start.2
  66.0 0.1 reshape.166
  66.1 0.6 copy-done.2
  66.7 0.5 broadcast.73
  67.2 2.3 %reduce.4 = f32[2,65536]{1,0:T(2,128)S(1)} reduce(f32[2,1,65536]{2,1,0:T(1,128)S(1)} %all-to-all-done.1, f32[]{:T(128)} %broadcast.73), dimensions={1}, to_apply=%all_to_all.7.reduce_sub_computation | reduce | bytes 1048580 | tf_op jit(solution)/shard_map/all_to_all | solution.py:18
  69.5 0.6 reshape.177
  70.1 1.9 %copy.16 = f32[1,8,2,64,2,64]{5,4,3,1,2,0:T(2,128)} copy(f32[1,8,2,64,2,64]{5,3,2,1,0,4:T(8,128)S(1)} %bitcast.100) | data formatting | bytes 1048576 | tf_op jit(solution)/shard_map/reshape | solution.py:19
  72.0 1.8 %reshape.161 = f32[1,8,2,64,128]{4,3,1,2,0:T(8,128)S(1)} reshape(f32[1,8,2,64,2,64]{5,4,3,1,2,0:T(2,128)} %copy.16) | data formatting | bytes 1048576 | tf_op jit(solution)/shard_map/reshape | solution.py:19
  73.8 0.1 broadcast_bitcast_fusion
  73.9 47.7 %all-to-all-done = f32[256,2,1,1,2,1,1,2,128]{8,7,4,1,6,5,3,2,0:T(2,128)S(1)} async-done(((f32[256,2,1,1,2,1,1,2,128]{8,7,4,1,6,5,3,2,0:T(2,128)}), f32[256,2,1,1,2,1,1,2,128]{8,7,4,1,6,5,3,2,0:T(2,128)S(1)}, u32[]{:S(2)}, u32[]{:S(2)}) %all-to-all-start) | async-done | bytes 1048608 | tf_op jit(solution)/shard_map/all_to_all | solution.py:40
  121.5 0.4 copy.13
  121.9 0.8 copy.14
  122.7 2.6 %gather_fusion = f32[512,2,256]{2,1,0:T(2,128)S(1)} fusion(f32[1,2,512,256]{3,1,2,0:T(2,128)S(1)} %copy.14, s32[512]{0:T(512)S(1)} %reshape.166), kind=kCustom, calls=%fused_computation | custom fusion | bytes 2101248 | tf_op jit(solution)/shard_map/vmap(jit(_take))/gather | solution.py:51
  125.3 0.1 copy.15
  125.4 0.1 broadcast_select_fusion
  125.5 0.6 fusion.12
  126.2 0.6 fusion.8
  126.8 0.6 fusion.2
  127.5 0.4 fusion.19
  127.8 0.4 fusion.18
  128.2 0.6 convolution_bitcast_fusion.2
  128.9 0.6 convolution_bitcast_fusion
  129.5 0.6 fusion.3
  130.1 0.4 fusion
  130.5 0.4 fusion.5
  131.0 0.6 fusion.6
  131.6 0.7 add_reduce_fusion
  132.3 0.1 stack.21
  132.4 0.1 stack.22
  132.5 20.4 %psum.21 = f32[128]{0:T(128)S(1)} all-reduce(f32[128]{0:T(128)S(1)} %get-tuple-element.5), channel_id=1, replica_groups=mesh['groups'=2,'range_0'=16,'range_1'=8,'sub'=2] {'range_0'}, use_global_device_ids=true, to_apply=%region_2.3 | all-reduce | flops 128 | bytes 1024 | tf_op jit(solution)/shard_map/psum | solution.py:46
  152.8 11.9 %psum.22 = f32[128]{0:T(128)S(1)} all-reduce(f32[128]{0:T(128)S(1)} %psum.21), channel_id=1, replica_groups=mesh['groups'=2,'range_0'=16,'range_1'=8,'sub'=2] {'range_1'}, use_global_device_ids=true, to_apply=%region_3.4 | all-reduce | flops 128 | bytes 1024 | tf_op jit(solution)/shard_map/psum | solution.py:46
  164.7 13.7 %psum.23 = f32[128]{0:T(128)S(1)} all-reduce(f32[128]{0:T(128)S(1)} %psum.22), channel_id=1, replica_groups=mesh['groups'=2,'range_0'=16,'range_1'=8,'sub'=2] {'sub'}, use_global_device_ids=true, to_apply=%region_4.5 | all-reduce | flops 128 | bytes 1024 | tf_op jit(solution)/shard_map/psum | solution.py:46
  178.4 0.5 broadcast_multiply_fusion.2
  178.9 0.8 pad_maximum_fusion.2
  179.8 0.8 pad_maximum_fusion.1
  (6 shorter events, 0.0 us)
Async XLA Ops:
  2.0 46.3 %copy-start = (f32[2,2,512,128]{3,2,1,0:T(8,128)S(1)}, f32[2,2,512,128]{3,2,1,0:T(8,128)}, u32[]{:S(2)}) copy-start(f32[2,2,512,128]{3,2,1,0:T(8,128)} %param.4) | copy-start | bytes 3145732
  3.4 46.3 %all-to-all-start.1 = ((f32[2,1,65536]{2,1,0:T(1,128)}), f32[2,1,65536]{2,1,0:T(1,128)S(1)}, u32[]{:S(2)}, u32[]{:S(2)}) async-start(f32[2,1,65536]{2,1,0:T(1,128)} %reshape.176), calls=%async_computation.1 | async-start | bytes 1048576 | tf_op jit(solution)/shard_map/all_to_all | solution.py:18
  49.7 16.2 %copy-start.1 = (s32[1,8,64]{2,1,0:T(8,128)S(1)}, s32[1,8,64]{2,1,0:T(8,128)}, u32[]{:S(2)}) copy-start(s32[1,8,64]{2,1,0:T(8,128)} %param.6) | copy-start | bytes 6148
  49.7 71.8 %all-to-all-start = ((f32[256,2,1,1,2,1,1,2,128]{8,7,4,1,6,5,3,2,0:T(2,128)}), f32[256,2,1,1,2,1,1,2,128]{8,7,4,1,6,5,3,2,0:T(2,128)S(1)}, u32[]{:S(2)}, u32[]{:S(2)}) async-start(f32[256,2,1,1,2,1,1,2,128]{8,7,4,1,6,5,3,2,0:T(2,128)} %bitcast.5), calls=%async_computation | async-start | bytes 2097152 | tf_op jit(solution)/shard_map/all_to_all | solution.py:40
  66.0 0.7 copy-start.2
